TPU v7x, 32 devices: a whole 2x2x4 slice. The times are simulated.
32 devices in a mesh: row: 4 (over y, x), col: 8 (over z, core).
Axes of the slice: x: 2, y: 2, z: 4, core: 2. Of those that a mesh axis runs over, the one named last changes fastest.
Arguments:
- matrix: float32 [2, 4, 256, 1, 8, 256], P(None, 'row', None, None, 'col'), as said below
Outputs:
- factored: float32 [2, 4, 256, 1, 8, 256], P(None, 'row', None, None, 'col')
Inputs may be any that keep to these rules, and one draw needn't show every extreme that they name: `matrix`: symmetric and positive definite.
All inputs are finite; a program needn't handle non-finite values.
Results may differ from a plain program's by a relative error of at most 0.0001.
Values sent between devices are 32-bit elements; how exact they have to be, the bound alone decides.
A program may use at most 128 MiB of HBM per device.

v0:
```python
import jax
import jax.numpy as jnp
from jax import lax
from jax.sharding import PartitionSpec as P

STEPS = 8


def broadcast(value, axis, source):
    kept = jnp.where(lax.axis_index(axis) == source, value, 0).astype(value.dtype)
    return lax.psum(kept, axis)


def solve_panel(factor, column):
    width = column.shape[1]
    inverse = jax.scipy.linalg.solve_triangular(
        factor, jnp.eye(width, dtype=jnp.float32), lower=True
    )
    solved = jnp.einsum("ts,ars->art", inverse, column, precision=lax.Precision.HIGHEST)
    return solved


def on_device(matrix):
    row_tiles = matrix.shape[0]
    width = matrix.shape[2]
    col_tiles = matrix.shape[3]
    tile_grid = matrix.reshape(row_tiles, width, col_tiles, width)
    num_row = lax.axis_size("row")
    num_col = lax.axis_size("col")
    my_row = lax.axis_index("row")
    my_col = lax.axis_index("col")
    rows_global = jnp.arange(row_tiles, dtype=jnp.int32) * num_row + my_row
    ratio = num_col // num_row
    for k in range(STEPS):
        lead_row = k % num_row
        lead_col = k % num_col
        local_row = k // num_row
        local_col = k // num_col
        column = tile_grid[:, :, local_col, :]
        candidate = tile_grid[local_row, :, local_col, :]
        keep = (rows_global > k)[:, None, None]
        diag_tile = broadcast(candidate, "row", lead_row)
        factor = jnp.linalg.cholesky(diag_tile)
        local_panel = jnp.where(keep, solve_panel(factor, column), 0.0)
        panel_rows = broadcast(local_panel, "col", lead_col)
        grouped = panel_rows.reshape(col_tiles, ratio, width, width)
        chosen = lax.dynamic_index_in_dim(grouped, my_col // num_row, 1, keepdims=False)
        panel_cols = broadcast(chosen, "row", my_col % num_row)
        update = jnp.einsum(
            "art,bst->arbs", panel_rows, panel_cols, precision=lax.Precision.HIGHEST
        )
        tile_grid = tile_grid - update
        diagonal_part = jnp.where((rows_global == k)[:, None, None], factor[None], 0.0)
        new_column = panel_rows + diagonal_part
        old_column = tile_grid[:, :, local_col, :]
        tile_grid = tile_grid.at[:, :, local_col, :].set(
            jnp.where(my_col == lead_col, new_column, old_column)
        )
    return tile_grid.reshape(matrix.shape)


def solution(mesh):
    placed = (P(None, "row", None, None, "col", None),)
    return jax.shard_map(
        on_device,
        mesh=mesh,
        in_specs=placed,
        out_specs=P(None, "row", None, None, "col", None),
        check_vma=False,
    )
```

profile of v0, /device:TPU:0, one launch (start us, length us, event | category | flops | bytes accessed | tf_op | source)
XLA Modules:
  0.0 1724.1 jit_solution(9675084317404435007)
XLA Ops:
  9.2 46.9 %all-reduce.26.cloned.1.call-done = f32[256,256]{0,1:T(8,128)} async-done(((f32[256,256]{0,1:T(8,128)}), f32[256,256]{0,1:T(8,128)}) %all-reduce.26.cloned.1.call-update) | async-done | bytes 262160 | tf_op jit(solution)/shard_map/psum | solution.py:11
  97.4 19.9 %custom-call.26 = f32[2,128,128]{1,2,0:T(8,128)S(1)} custom-call(f32[2,128,128]{2,1,0:T(8,128)S(1)} %get-tuple-element.153), custom_call_target="InvertDiagBlocksLowerTriangular" | custom-call | tf_op jit(solution)/shard_map/jit(_solve_triangular)/triangular_solve | solution.py:16
  119.8 56.6 %all-reduce.28.cloned.1.call-done = f32[2,256,256]{1,2,0:T(8,128)} async-done(((f32[2,256,256]{1,2,0:T(8,128)}), f32[2,256,256]{1,2,0:T(8,128)}) %all-reduce.28.cloned.1.call-update) | async-done | bytes 524304 | tf_op jit(solution)/shard_map/psum | solution.py:11
  178.6 42.8 %all-reduce.30.cloned.1.call-done = f32[256,256]{0,1:T(8,128)} async-done(((f32[256,256]{0,1:T(8,128)}), f32[256,256]{0,1:T(8,128)}) %all-reduce.30.cloned.1.call-update) | async-done | bytes 262160 | tf_op jit(solution)/shard_map/psum | solution.py:11
  223.9 43.4 %all-reduce.32.cloned.1.call-done = f32[256,256]{0,1:T(8,128)} async-done(((f32[256,256]{0,1:T(8,128)}), f32[256,256]{0,1:T(8,128)}) %all-reduce.32.cloned.1.call-update) | async-done | bytes 262160 | tf_op jit(solution)/shard_map/psum | solution.py:11
  319.8 19.7 %custom-call.28 = f32[2,128,128]{1,2,0:T(8,128)S(1)} custom-call(f32[2,128,128]{2,1,0:T(8,128)S(1)} %get-tuple-element.154), custom_call_target="InvertDiagBlocksLowerTriangular" | custom-call | tf_op jit(solution)/shard_map/jit(_solve_triangular)/triangular_solve | solution.py:16
  341.8 56.6 %all-reduce.34.cloned.1.call-done = f32[2,256,256]{1,2,0:T(8,128)} async-done(((f32[2,256,256]{1,2,0:T(8,128)}), f32[2,256,256]{1,2,0:T(8,128)}) %all-reduce.34.cloned.1.call-update) | async-done | bytes 524304 | tf_op jit(solution)/shard_map/psum | solution.py:11
  400.3 43.0 %all-reduce.36.cloned.1.call-done = f32[256,256]{0,1:T(8,128)} async-done(((f32[256,256]{0,1:T(8,128)}), f32[256,256]{0,1:T(8,128)}) %all-reduce.36.cloned.1.call-update) | async-done | bytes 262160 | tf_op jit(solution)/shard_map/psum | solution.py:11
  445.8 43.5 %all-reduce.38.cloned.1.call-done = f32[256,256]{0,1:T(8,128)} async-done(((f32[256,256]{0,1:T(8,128)}), f32[256,256]{0,1:T(8,128)}) %all-reduce.38.cloned.1.call-update) | async-done | bytes 262160 | tf_op jit(solution)/shard_map/psum | solution.py:11
  531.7 19.7 %custom-call.30 = f32[2,128,128]{1,2,0:T(8,128)S(1)} custom-call(f32[2,128,128]{2,1,0:T(8,128)S(1)} %get-tuple-element.155), custom_call_target="InvertDiagBlocksLowerTriangular" | custom-call | tf_op jit(solution)/shard_map/jit(_solve_triangular)/triangular_solve | solution.py:16
  553.8 56.6 %all-reduce.40.cloned.1.call-done = f32[2,256,256]{1,2,0:T(8,128)} async-done(((f32[2,256,256]{1,2,0:T(8,128)}), f32[2,256,256]{1,2,0:T(8,128)}) %all-reduce.40.cloned.1.call-update) | async-done | bytes 524304 | tf_op jit(solution)/shard_map/psum | solution.py:11
  612.3 43.2 %all-reduce.42.cloned.1.call-done = f32[256,256]{0,1:T(8,128)} async-done(((f32[256,256]{0,1:T(8,128)}), f32[256,256]{0,1:T(8,128)}) %all-reduce.42.cloned.1.call-update) | async-done | bytes 262160 | tf_op jit(solution)/shard_map/psum | solution.py:11
  657.9 43.4 %all-reduce.44.cloned.1.call-done = f32[256,256]{0,1:T(8,128)} async-done(((f32[256,256]{0,1:T(8,128)}), f32[256,256]{0,1:T(8,128)}) %all-reduce.44.cloned.1.call-update) | async-done | bytes 262160 | tf_op jit(solution)/shard_map/psum | solution.py:11
  743.4 19.7 %custom-call.32 = f32[2,128,128]{1,2,0:T(8,128)S(1)} custom-call(f32[2,128,128]{2,1,0:T(8,128)S(1)} %get-tuple-element.156), custom_call_target="InvertDiagBlocksLowerTriangular" | custom-call | tf_op jit(solution)/shard_map/jit(_solve_triangular)/triangular_solve | solution.py:16
  765.5 56.6 %all-reduce.46.cloned.1.call-done = f32[2,256,256]{1,2,0:T(8,128)} async-done(((f32[2,256,256]{1,2,0:T(8,128)}), f32[2,256,256]{1,2,0:T(8,128)}) %all-reduce.46.cloned.1.call-update) | async-done | bytes 524304 | tf_op jit(solution)/shard_map/psum | solution.py:11
  824.0 43.0 %all-reduce.48.cloned.1.call-done = f32[256,256]{0,1:T(8,128)} async-done(((f32[256,256]{0,1:T(8,128)}), f32[256,256]{0,1:T(8,128)}) %all-reduce.48.cloned.1.call-update) | async-done | bytes 262160 | tf_op jit(solution)/shard_map/psum | solution.py:11
  869.5 43.5 %all-reduce.50.cloned.1.call-done = f32[256,256]{0,1:T(8,128)} async-done(((f32[256,256]{0,1:T(8,128)}), f32[256,256]{0,1:T(8,128)}) %all-reduce.50.cloned.1.call-update) | async-done | bytes 262160 | tf_op jit(solution)/shard_map/psum | solution.py:11
  955.3 19.7 %custom-call.34 = f32[2,128,128]{1,2,0:T(8,128)S(1)} custom-call(f32[2,128,128]{2,1,0:T(8,128)S(1)} %get-tuple-element.157), custom_call_target="InvertDiagBlocksLowerTriangular" | custom-call | tf_op jit(solution)/shard_map/jit(_solve_triangular)/triangular_solve | solution.py:16
  977.4 56.7 %all-reduce.52.cloned.1.call-done = f32[2,256,256]{1,2,0:T(8,128)} async-done(((f32[2,256,256]{1,2,0:T(8,128)}), f32[2,256,256]{1,2,0:T(8,128)}) %all-reduce.52.cloned.1.call-update) | async-done | bytes 524304 | tf_op jit(solution)/shard_map/psum | solution.py:11
  1036.0 43.0 %all-reduce.54.cloned.1.call-done = f32[256,256]{0,1:T(8,128)} async-done(((f32[256,256]{0,1:T(8,128)}), f32[256,256]{0,1:T(8,128)}) %all-reduce.54.cloned.1.call-update) | async-done | bytes 262160 | tf_op jit(solution)/shard_map/psum | solution.py:11
  1081.4 43.4 %all-reduce.56.cloned.1.call-done = f32[256,256]{0,1:T(8,128)} async-done(((f32[256,256]{0,1:T(8,128)}), f32[256,256]{0,1:T(8,128)}) %all-reduce.56.cloned.1.call-update) | async-done | bytes 262160 | tf_op jit(solution)/shard_map/psum | solution.py:11
  1166.9 19.7 %custom-call.36 = f32[2,128,128]{1,2,0:T(8,128)S(1)} custom-call(f32[2,128,128]{2,1,0:T(8,128)S(1)} %get-tuple-element.158), custom_call_target="InvertDiagBlocksLowerTriangular" | custom-call | tf_op jit(solution)/shard_map/jit(_solve_triangular)/triangular_solve | solution.py:16
  1189.0 56.6 %all-reduce.58.cloned.1.call-done = f32[2,256,256]{1,2,0:T(8,128)} async-done(((f32[2,256,256]{1,2,0:T(8,128)}), f32[2,256,256]{1,2,0:T(8,128)}) %all-reduce.58.cloned.1.call-update) | async-done | bytes 524304 | tf_op jit(solution)/shard_map/psum | solution.py:11
  1247.5 43.0 %all-reduce.60.cloned.1.call-done = f32[256,256]{0,1:T(8,128)} async-done(((f32[256,256]{0,1:T(8,128)}), f32[256,256]{0,1:T(8,128)}) %all-reduce.60.cloned.1.call-update) | async-done | bytes 262160 | tf_op jit(solution)/shard_map/psum | solution.py:11
  1293.0 43.5 %all-reduce.62.cloned.1.call-done = f32[256,256]{0,1:T(8,128)} async-done(((f32[256,256]{0,1:T(8,128)}), f32[256,256]{0,1:T(8,128)}) %all-reduce.62.cloned.1.call-update) | async-done | bytes 262160 | tf_op jit(solution)/shard_map/psum | solution.py:11
  1378.6 19.7 %custom-call.38 = f32[2,128,128]{1,2,0:T(8,128)S(1)} custom-call(f32[2,128,128]{2,1,0:T(8,128)S(1)} %get-tuple-element.159), custom_call_target="InvertDiagBlocksLowerTriangular" | custom-call | tf_op jit(solution)/shard_map/jit(_solve_triangular)/triangular_solve | solution.py:16
  1400.7 56.6 %all-reduce.64.cloned.1.call-done = f32[2,256,256]{1,2,0:T(8,128)} async-done(((f32[2,256,256]{1,2,0:T(8,128)}), f32[2,256,256]{1,2,0:T(8,128)}) %all-reduce.64.cloned.1.call-update) | async-done | bytes 524304 | tf_op jit(solution)/shard_map/psum | solution.py:11
  1459.2 43.2 %all-reduce.66.cloned.1.call-done = f32[256,256]{0,1:T(8,128)} async-done(((f32[256,256]{0,1:T(8,128)}), f32[256,256]{0,1:T(8,128)}) %all-reduce.66.cloned.1.call-update) | async-done | bytes 262160 | tf_op jit(solution)/shard_map/psum | solution.py:11
  1504.9 43.5 %all-reduce.68.cloned.1.call-done = f32[256,256]{0,1:T(8,128)} async-done(((f32[256,256]{0,1:T(8,128)}), f32[256,256]{0,1:T(8,128)}) %all-reduce.68.cloned.1.call-update) | async-done | bytes 262160 | tf_op jit(solution)/shard_map/psum | solution.py:11
  1590.5 19.7 %custom-call.40 = f32[2,128,128]{1,2,0:T(8,128)S(1)} custom-call(f32[2,128,128]{2,1,0:T(8,128)S(1)} %get-tuple-element.160), custom_call_target="InvertDiagBlocksLowerTriangular" | custom-call | tf_op jit(solution)/shard_map/jit(_solve_triangular)/triangular_solve | solution.py:16
  1612.6 56.6 %all-reduce.70.cloned.1.call-done = f32[2,256,256]{1,2,0:T(8,128)} async-done(((f32[2,256,256]{1,2,0:T(8,128)}), f32[2,256,256]{1,2,0:T(8,128)}) %all-reduce.70.cloned.1.call-update) | async-done | bytes 524304 | tf_op jit(solution)/shard_map/psum | solution.py:11
  1671.1 43.1 %all-reduce.72.cloned.1.call-done = f32[256,256]{0,1:T(8,128)} async-done(((f32[256,256]{0,1:T(8,128)}), f32[256,256]{0,1:T(8,128)}) %all-reduce.72.cloned.1.call-update) | async-done | bytes 262160 | tf_op jit(solution)/shard_map/psum | solution.py:11
  (346 shorter events, 424.6 us)
Async XLA Ops:
  6.5 49.5 %all-reduce.26.cloned.1.call-start = ((), (), s32[]{:S(2)}) async-start(), calls=%async_computation | async-start | bytes 524288 | tf_op jit(solution)/shard_map/psum | solution.py:11
  8.4 167.9 %all-reduce.28.cloned.1.call-start = ((), (), s32[]{:S(2)}) async-start(), calls=%async_computation.1 | async-start | bytes 1048576 | tf_op jit(solution)/shard_map/psum | solution.py:11
  119.7 101.7 %all-reduce.30.cloned.1.call-start = ((), (), s32[]{:S(2)}) async-start(), calls=%async_computation.2 | async-start | bytes 524288 | tf_op jit(solution)/shard_map/psum | solution.py:11
  178.0 89.2 %all-reduce.32.cloned.1.call-start = ((), (), s32[]{:S(2)}) async-start(), calls=%async_computation.3 | async-start | bytes 524288 | tf_op jit(solution)/shard_map/psum | solution.py:11
  178.4 43.0 %copy-start.1 = (f32[2,256,256]{1,2,0:T(8,128)S(1)}, f32[2,256,256]{1,2,0:T(8,128)}, u32[]{:S(2)}) copy-start(f32[2,256,256]{1,2,0:T(8,128)} %all-reduce.28.cloned.1.call-done) | copy-start | bytes 1572868
  223.8 174.6 %all-reduce.34.cloned.1.call-start = ((), (), s32[]{:S(2)}) async-start(), calls=%async_computation.4 | async-start | bytes 1048576 | tf_op jit(solution)/shard_map/psum | solution.py:11
  341.8 101.6 %all-reduce.36.cloned.1.call-start = ((), (), s32[]{:S(2)}) async-start(), calls=%async_computation.5 | async-start | bytes 524288 | tf_op jit(solution)/shard_map/psum | solution.py:11
  400.1 43.2 %copy-start.2 = (f32[2,256,256]{1,2,0:T(8,128)S(1)}, f32[2,256,256]{1,2,0:T(8,128)}, u32[]{:S(2)}) copy-start(f32[2,256,256]{1,2,0:T(8,128)} %all-reduce.34.cloned.1.call-done) | copy-start | bytes 1572868
  400.1 89.2 %all-reduce.38.cloned.1.call-start = ((), (), s32[]{:S(2)}) async-start(), calls=%async_computation.6 | async-start | bytes 524288 | tf_op jit(solution)/shard_map/psum | solution.py:11
  445.8 164.6 %all-reduce.40.cloned.1.call-start = ((), (), s32[]{:S(2)}) async-start(), calls=%async_computation.7 | async-start | bytes 1048576 | tf_op jit(solution)/shard_map/psum | solution.py:11
  553.7 101.8 %all-reduce.42.cloned.1.call-start = ((), (), s32[]{:S(2)}) async-start(), calls=%async_computation.8 | async-start | bytes 524288 | tf_op jit(solution)/shard_map/psum | solution.py:11
  612.1 43.4 %copy-start.3 = (f32[2,256,256]{1,2,0:T(8,128)S(1)}, f32[2,256,256]{1,2,0:T(8,128)}, u32[]{:S(2)}) copy-start(f32[2,256,256]{1,2,0:T(8,128)} %all-reduce.40.cloned.1.call-done) | copy-start | bytes 1572868
  612.1 89.2 %all-reduce.44.cloned.1.call-start = ((), (), s32[]{:S(2)}) async-start(), calls=%async_computation.9 | async-start | bytes 524288 | tf_op jit(solution)/shard_map/psum | solution.py:11
  657.9 164.2 %all-reduce.46.cloned.1.call-start = ((), (), s32[]{:S(2)}) async-start(), calls=%async_computation.10 | async-start | bytes 1048576 | tf_op jit(solution)/shard_map/psum | solution.py:11
  765.5 101.6 %all-reduce.48.cloned.1.call-start = ((), (), s32[]{:S(2)}) async-start(), calls=%async_computation.11 | async-start | bytes 524288 | tf_op jit(solution)/shard_map/psum | solution.py:11
  823.8 43.2 %copy-start.5 = (f32[2,256,256]{1,2,0:T(8,128)S(1)}, f32[2,256,256]{1,2,0:T(8,128)}, u32[]{:S(2)}) copy-start(f32[2,256,256]{1,2,0:T(8,128)} %all-reduce.46.cloned.1.call-done) | copy-start | bytes 1572868
  823.8 89.2 %all-reduce.50.cloned.1.call-start = ((), (), s32[]{:S(2)}) async-start(), calls=%async_computation.12 | async-start | bytes 524288 | tf_op jit(solution)/shard_map/psum | solution.py:11
  869.4 164.6 %all-reduce.52.cloned.1.call-start = ((), (), s32[]{:S(2)}) async-start(), calls=%async_computation.13 | async-start | bytes 1048576 | tf_op jit(solution)/shard_map/psum | solution.py:11
  977.4 101.6 %all-reduce.54.cloned.1.call-start = ((), (), s32[]{:S(2)}) async-start(), calls=%async_computation.14 | async-start | bytes 524288 | tf_op jit(solution)/shard_map/psum | solution.py:11
  1035.7 43.2 %copy-start.6 = (f32[2,256,256]{1,2,0:T(8,128)S(1)}, f32[2,256,256]{1,2,0:T(8,128)}, u32[]{:S(2)}) copy-start(f32[2,256,256]{1,2,0:T(8,128)} %all-reduce.52.cloned.1.call-done) | copy-start | bytes 1572868
  1035.8 89.0 %all-reduce.56.cloned.1.call-start = ((), (), s32[]{:S(2)}) async-start(), calls=%async_computation.15 | async-start | bytes 524288 | tf_op jit(solution)/shard_map/psum | solution.py:11
  1081.4 164.2 %all-reduce.58.cloned.1.call-start = ((), (), s32[]{:S(2)}) async-start(), calls=%async_computation.16 | async-start | bytes 1048576 | tf_op jit(solution)/shard_map/psum | solution.py:11
  1188.9 101.6 %all-reduce.60.cloned.1.call-start = ((), (), s32[]{:S(2)}) async-start(), calls=%async_computation.17 | async-start | bytes 524288 | tf_op jit(solution)/shard_map/psum | solution.py:11
  1247.3 43.2 %copy-start.7 = (f32[2,256,256]{1,2,0:T(8,128)S(1)}, f32[2,256,256]{1,2,0:T(8,128)}, u32[]{:S(2)}) copy-start(f32[2,256,256]{1,2,0:T(8,128)} %all-reduce.58.cloned.1.call-done) | copy-start | bytes 1572868
  1247.3 89.2 %all-reduce.62.cloned.1.call-start = ((), (), s32[]{:S(2)}) async-start(), calls=%async_computation.18 | async-start | bytes 524288 | tf_op jit(solution)/shard_map/psum | solution.py:11
  1292.9 164.4 %all-reduce.64.cloned.1.call-start = ((), (), s32[]{:S(2)}) async-start(), calls=%async_computation.19 | async-start | bytes 1048576 | tf_op jit(solution)/shard_map/psum | solution.py:11
  1400.7 101.7 %all-reduce.66.cloned.1.call-start = ((), (), s32[]{:S(2)}) async-start(), calls=%async_computation.20 | async-start | bytes 524288 | tf_op jit(solution)/shard_map/psum | solution.py:11
  1459.0 43.4 %copy-start.8 = (f32[2,256,256]{1,2,0:T(8,128)S(1)}, f32[2,256,256]{1,2,0:T(8,128)}, u32[]{:S(2)}) copy-start(f32[2,256,256]{1,2,0:T(8,128)} %all-reduce.64.cloned.1.call-done) | copy-start | bytes 1572868
  1459.0 89.3 %all-reduce.68.cloned.1.call-start = ((), (), s32[]{:S(2)}) async-start(), calls=%async_computation.21 | async-start | bytes 524288 | tf_op jit(solution)/shard_map/psum | solution.py:11
  1504.8 164.4 %all-reduce.70.cloned.1.call-start = ((), (), s32[]{:S(2)}) async-start(), calls=%async_computation.22 | async-start | bytes 1048576 | tf_op jit(solution)/shard_map/psum | solution.py:11
  1612.6 101.5 %all-reduce.72.cloned.1.call-start = ((), (), s32[]{:S(2)}) async-start(), calls=%async_computation.23 | async-start | bytes 524288 | tf_op jit(solution)/shard_map/psum | solution.py:11
  1670.9 43.2 %copy-start.4 = (f32[2,256,256]{1,2,0:T(8,128)S(1)}, f32[2,256,256]{1,2,0:T(8,128)}, u32[]{:S(2)}) copy-start(f32[2,256,256]{1,2,0:T(8,128)} %all-reduce.70.cloned.1.call-done) | copy-start | bytes 1572868
  (10 other events, 11.4 us)
Sparse Core Ops, SparseCore 0:
  10.3 45.7 all-reduce.25
  119.8 56.4 all-reduce.27
  179.3 42.0 all-reduce.29
  224.2 43.0 all-reduce.31
  341.9 56.4 all-reduce.33
  401.2 42.0 all-reduce.35
  446.3 43.0 all-reduce.37
  553.8 56.5 all-reduce.39
  613.3 42.0 all-reduce.41
  658.2 43.0 all-reduce.43
  765.6 56.4 all-reduce.45
  824.9 42.0 all-reduce.47
  869.9 43.0 all-reduce.49
  977.5 56.5 all-reduce.51
  1036.8 42.0 all-reduce.53
  1081.7 43.0 all-reduce.55
  1189.1 56.4 all-reduce.57
  1248.4 42.0 all-reduce.59
  1293.4 43.0 all-reduce.61
  1400.8 56.5 all-reduce.63
  1460.2 42.0 all-reduce.65
  1505.3 43.0 all-reduce.67
  1612.7 56.4 all-reduce.69
  1672.0 42.0 all-reduce.71
where the time goes:
time: 1730 us; the launch traced here: 1720 us
  waiting for transfers between devices  1150 us (66%)
  other arithmetic  454 us (26%)
  local copies, waits for them, and re-layouts  46.2 us (3%)
  matrix products  35.5 us (2%)
  between operations  26.2 us (2%)
    psum x24, waiting for transfers between devices, broadcast(): return lax.psum(kept, axis)  1150 us
    another operation x55, other arithmetic, on_device(): factor = jnp.linalg.cholesky(diag_tile)  277 us
    another operation x17, other arithmetic, solve_panel(): jax.scipy.linalg.solve_triangular(factor, jnp.eye(width, dtype=jnp.float3...  158 us
  transfers between devices with their start and end apart: 24, of which 24 were waited for; matrix products, arithmetic and copies ran while one was open for 0% of the time, Pallas kernels for 0%

commit v1 on v0

--- a/solution.py
+++ b/solution.py
@@ -8,7 +8,7 @@
 
 def broadcast(value, axis, source):
     kept = jnp.where(lax.axis_index(axis) == source, value, 0).astype(value.dtype)
-    return lax.psum(kept, axis)
+    return jnp.sum(lax.all_gather(kept, axis), axis=0)
 
 
 def solve_panel(factor, column):

time: 1730 us -> 1400 us (0.81)
  waiting for transfers between devices: 1150 us -> 795 us
  other arithmetic: 454 us -> 488 us
    psum x24 -> x0, waiting for transfers between devices: 1150 us -> none  [broadcast(): return lax.psum(kept, axis)]
    all_gather x0 -> x24, waiting for transfers between devices: none -> 795 us  [broadcast(): return jnp.sum(lax.all_gather(kept, axis), axis=0)]
    reduce_sum x0 -> x23, other arithmetic: none -> 38.7 us  [broadcast(): return jnp.sum(lax.all_gather(kept, axis), axis=0)]
where the time goes in v1:
time: 1400 us; the launch traced here: 1390 us
  waiting for transfers between devices  795 us (57%)
  other arithmetic  488 us (35%)
  local copies, waits for them, and re-layouts  37.4 us (3%)
  matrix products  26.3 us (2%)
  between operations  26.1 us (2%)
    all_gather x24, waiting for transfers between devices, broadcast(): return jnp.sum(lax.all_gather(kept, axis), axis=0)  795 us
    another operation x55, other arithmetic, on_device(): factor = jnp.linalg.cholesky(diag_tile)  277 us
    another operation x17, other arithmetic, solve_panel(): jax.scipy.linalg.solve_triangular(factor, jnp.eye(width, dtype=jnp.float3...  158 us
    reduce_sum x23, other arithmetic, broadcast(): return jnp.sum(lax.all_gather(kept, axis), axis=0)  38.7 us
    another operation x57, local copies, waits for them, and re-layouts, solve_panel(): jax.scipy.linalg.solve_triangular(factor, jnp.eye(width, dtype=jnp.float3...  32.6 us
  transfers between devices with their start and end apart: 24, of which 24 were waited for; matrix products, arithmetic and copies ran while one was open for 0% of the time, Pallas kernels for 0%

profile of v1, /device:TPU:0, one launch (start us, length us, event | category | flops | bytes accessed | tf_op | source)
XLA Modules:
  0.0 1386.7 jit_solution(12965815197017878945)
XLA Ops:
  8.6 29.8 %all-gather.56.cloned.1.call-done = f32[4,1,256,1,1,256]{5,2,4,3,1,0:T(8,128)} async-done(((f32[1,1,256,1,1,256]{5,2,4,3,1,0:T(8,128)}), f32[4,1,256,1,1,256]{5,2,4,3,1,0:T(8,128)}) %all-gather.56.cloned.1.call-update) | async-done | bytes 1048592 | tf_op jit(solution)/shard_map/all_gather | solution.py:11
  80.3 19.7 %custom-call.26 = f32[2,128,128]{1,2,0:T(8,128)S(1)} custom-call(f32[2,128,128]{2,1,0:T(8,128)S(1)} %get-tuple-element.153), custom_call_target="InvertDiagBlocksLowerTriangular" | custom-call | tf_op jit(solution)/shard_map/jit(_solve_triangular)/triangular_solve | solution.py:16
  102.7 46.9 %all-gather.58.cloned.1.call-done = f32[16,256,256]{2,1,0:T(8,128)} async-done(((f32[2,256,256]{2,1,0:T(8,128)}), f32[16,256,256]{2,1,0:T(8,128)}) %all-gather.58.cloned.1.call-update) | async-done | bytes 4194320 | tf_op jit(solution)/shard_map/all_gather | solution.py:11
  153.0 25.4 %all-gather.60.cloned.1.call-done = f32[4,256,256]{2,1,0:T(8,128)} async-done(((f32[1,256,256]{2,1,0:T(8,128)}), f32[4,256,256]{2,1,0:T(8,128)}) %all-gather.60.cloned.1.call-update) | async-done | bytes 1048592 | tf_op jit(solution)/shard_map/all_gather | solution.py:11
  181.1 26.6 %all-gather.42.cloned.1.call-done = f32[4,256,256]{2,1,0:T(8,128)} async-done(((f32[1,256,256]{2,1,0:T(8,128)}), f32[4,256,256]{2,1,0:T(8,128)}) %all-gather.42.cloned.1.call-update) | async-done | bytes 1048592 | tf_op jit(solution)/shard_map/all_gather | solution.py:11
  260.7 19.7 %custom-call.28 = f32[2,128,128]{1,2,0:T(8,128)S(1)} custom-call(f32[2,128,128]{2,1,0:T(8,128)S(1)} %get-tuple-element.154), custom_call_target="InvertDiagBlocksLowerTriangular" | custom-call | tf_op jit(solution)/shard_map/jit(_solve_triangular)/triangular_solve | solution.py:16
  282.8 47.0 %all-gather.62.cloned.1.call-done = f32[16,256,256]{2,1,0:T(8,128)} async-done(((f32[2,256,256]{2,1,0:T(8,128)}), f32[16,256,256]{2,1,0:T(8,128)}) %all-gather.62.cloned.1.call-update) | async-done | bytes 4194320 | tf_op jit(solution)/shard_map/all_gather | solution.py:11
  333.1 25.4 %all-gather.64.cloned.1.call-done = f32[4,256,256]{2,1,0:T(8,128)} async-done(((f32[1,256,256]{2,1,0:T(8,128)}), f32[4,256,256]{2,1,0:T(8,128)}) %all-gather.64.cloned.1.call-update) | async-done | bytes 1048592 | tf_op jit(solution)/shard_map/all_gather | solution.py:11
  361.3 26.6 %all-gather.44.cloned.1.call-done = f32[4,256,256]{2,1,0:T(8,128)} async-done(((f32[1,256,256]{2,1,0:T(8,128)}), f32[4,256,256]{2,1,0:T(8,128)}) %all-gather.44.cloned.1.call-update) | async-done | bytes 1048592 | tf_op jit(solution)/shard_map/all_gather | solution.py:11
  430.4 19.7 %custom-call.30 = f32[2,128,128]{1,2,0:T(8,128)S(1)} custom-call(f32[2,128,128]{2,1,0:T(8,128)S(1)} %get-tuple-element.155), custom_call_target="InvertDiagBlocksLowerTriangular" | custom-call | tf_op jit(solution)/shard_map/jit(_solve_triangular)/triangular_solve | solution.py:16
  452.5 47.0 %all-gather.66.cloned.1.call-done = f32[16,256,256]{2,1,0:T(8,128)} async-done(((f32[2,256,256]{2,1,0:T(8,128)}), f32[16,256,256]{2,1,0:T(8,128)}) %all-gather.66.cloned.1.call-update) | async-done | bytes 4194320 | tf_op jit(solution)/shard_map/all_gather | solution.py:11
  502.8 25.4 %all-gather.68.cloned.1.call-done = f32[4,256,256]{2,1,0:T(8,128)} async-done(((f32[1,256,256]{2,1,0:T(8,128)}), f32[4,256,256]{2,1,0:T(8,128)}) %all-gather.68.cloned.1.call-update) | async-done | bytes 1048592 | tf_op jit(solution)/shard_map/all_gather | solution.py:11
  531.0 26.6 %all-gather.46.cloned.1.call-done = f32[4,256,256]{2,1,0:T(8,128)} async-done(((f32[1,256,256]{2,1,0:T(8,128)}), f32[4,256,256]{2,1,0:T(8,128)}) %all-gather.46.cloned.1.call-update) | async-done | bytes 1048592 | tf_op jit(solution)/shard_map/all_gather | solution.py:11
  600.0 19.7 %custom-call.32 = f32[2,128,128]{1,2,0:T(8,128)S(1)} custom-call(f32[2,128,128]{2,1,0:T(8,128)S(1)} %get-tuple-element.156), custom_call_target="InvertDiagBlocksLowerTriangular" | custom-call | tf_op jit(solution)/shard_map/jit(_solve_triangular)/triangular_solve | solution.py:16
  622.0 47.0 %all-gather.70.cloned.1.call-done = f32[16,256,256]{2,1,0:T(8,128)} async-done(((f32[2,256,256]{2,1,0:T(8,128)}), f32[16,256,256]{2,1,0:T(8,128)}) %all-gather.70.cloned.1.call-update) | async-done | bytes 4194320 | tf_op jit(solution)/shard_map/all_gather | solution.py:11
  672.4 25.4 %all-gather.72.cloned.1.call-done = f32[4,256,256]{2,1,0:T(8,128)} async-done(((f32[1,256,256]{2,1,0:T(8,128)}), f32[4,256,256]{2,1,0:T(8,128)}) %all-gather.72.cloned.1.call-update) | async-done | bytes 1048592 | tf_op jit(solution)/shard_map/all_gather | solution.py:11
  700.5 26.6 %all-gather.48.cloned.1.call-done = f32[4,256,256]{2,1,0:T(8,128)} async-done(((f32[1,256,256]{2,1,0:T(8,128)}), f32[4,256,256]{2,1,0:T(8,128)}) %all-gather.48.cloned.1.call-update) | async-done | bytes 1048592 | tf_op jit(solution)/shard_map/all_gather | solution.py:11
  769.7 19.7 %custom-call.34 = f32[2,128,128]{1,2,0:T(8,128)S(1)} custom-call(f32[2,128,128]{2,1,0:T(8,128)S(1)} %get-tuple-element.157), custom_call_target="InvertDiagBlocksLowerTriangular" | custom-call | tf_op jit(solution)/shard_map/jit(_solve_triangular)/triangular_solve | solution.py:16
  791.8 47.0 %all-gather.74.cloned.1.call-done = f32[16,256,256]{2,1,0:T(8,128)} async-done(((f32[2,256,256]{2,1,0:T(8,128)}), f32[16,256,256]{2,1,0:T(8,128)}) %all-gather.74.cloned.1.call-update) | async-done | bytes 4194320 | tf_op jit(solution)/shard_map/all_gather | solution.py:11
  842.1 25.4 %all-gather.76.cloned.1.call-done = f32[4,256,256]{2,1,0:T(8,128)} async-done(((f32[1,256,256]{2,1,0:T(8,128)}), f32[4,256,256]{2,1,0:T(8,128)}) %all-gather.76.cloned.1.call-update) | async-done | bytes 1048592 | tf_op jit(solution)/shard_map/all_gather | solution.py:11
  870.3 26.6 %all-gather.50.cloned.1.call-done = f32[4,256,256]{2,1,0:T(8,128)} async-done(((f32[1,256,256]{2,1,0:T(8,128)}), f32[4,256,256]{2,1,0:T(8,128)}) %all-gather.50.cloned.1.call-update) | async-done | bytes 1048592 | tf_op jit(solution)/shard_map/all_gather | solution.py:11
  939.2 19.7 %custom-call.36 = f32[2,128,128]{1,2,0:T(8,128)S(1)} custom-call(f32[2,128,128]{2,1,0:T(8,128)S(1)} %get-tuple-element.158), custom_call_target="InvertDiagBlocksLowerTriangular" | custom-call | tf_op jit(solution)/shard_map/jit(_solve_triangular)/triangular_solve | solution.py:16
  961.3 47.0 %all-gather.78.cloned.1.call-done = f32[16,256,256]{2,1,0:T(8,128)} async-done(((f32[2,256,256]{2,1,0:T(8,128)}), f32[16,256,256]{2,1,0:T(8,128)}) %all-gather.78.cloned.1.call-update) | async-done | bytes 4194320 | tf_op jit(solution)/shard_map/all_gather | solution.py:11
  1011.6 25.4 %all-gather.80.cloned.1.call-done = f32[4,256,256]{2,1,0:T(8,128)} async-done(((f32[1,256,256]{2,1,0:T(8,128)}), f32[4,256,256]{2,1,0:T(8,128)}) %all-gather.80.cloned.1.call-update) | async-done | bytes 1048592 | tf_op jit(solution)/shard_map/all_gather | solution.py:11
  1039.8 26.6 %all-gather.52.cloned.1.call-done = f32[4,256,256]{2,1,0:T(8,128)} async-done(((f32[1,256,256]{2,1,0:T(8,128)}), f32[4,256,256]{2,1,0:T(8,128)}) %all-gather.52.cloned.1.call-update) | async-done | bytes 1048592 | tf_op jit(solution)/shard_map/all_gather | solution.py:11
  1108.8 19.7 %custom-call.38 = f32[2,128,128]{1,2,0:T(8,128)S(1)} custom-call(f32[2,128,128]{2,1,0:T(8,128)S(1)} %get-tuple-element.159), custom_call_target="InvertDiagBlocksLowerTriangular" | custom-call | tf_op jit(solution)/shard_map/jit(_solve_triangular)/triangular_solve | solution.py:16
  1130.9 47.0 %all-gather.82.cloned.1.call-done = f32[16,256,256]{2,1,0:T(8,128)} async-done(((f32[2,256,256]{2,1,0:T(8,128)}), f32[16,256,256]{2,1,0:T(8,128)}) %all-gather.82.cloned.1.call-update) | async-done | bytes 4194320 | tf_op jit(solution)/shard_map/all_gather | solution.py:11
  1181.2 25.4 %all-gather.84.cloned.1.call-done = f32[4,256,256]{2,1,0:T(8,128)} async-done(((f32[1,256,256]{2,1,0:T(8,128)}), f32[4,256,256]{2,1,0:T(8,128)}) %all-gather.84.cloned.1.call-update) | async-done | bytes 1048592 | tf_op jit(solution)/shard_map/all_gather | solution.py:11
  1209.3 26.6 %all-gather.54.cloned.1.call-done = f32[4,256,256]{2,1,0:T(8,128)} async-done(((f32[1,256,256]{2,1,0:T(8,128)}), f32[4,256,256]{2,1,0:T(8,128)}) %all-gather.54.cloned.1.call-update) | async-done | bytes 1048592 | tf_op jit(solution)/shard_map/all_gather | solution.py:11
  1278.4 19.7 %custom-call.40 = f32[2,128,128]{1,2,0:T(8,128)S(1)} custom-call(f32[2,128,128]{2,1,0:T(8,128)S(1)} %get-tuple-element.160), custom_call_target="InvertDiagBlocksLowerTriangular" | custom-call | tf_op jit(solution)/shard_map/jit(_solve_triangular)/triangular_solve | solution.py:16
  1300.5 47.0 %all-gather.86.cloned.1.call-done = f32[16,256,256]{2,1,0:T(8,128)} async-done(((f32[2,256,256]{2,1,0:T(8,128)}), f32[16,256,256]{2,1,0:T(8,128)}) %all-gather.86.cloned.1.call-update) | async-done | bytes 4194320 | tf_op jit(solution)/shard_map/all_gather | solution.py:11
  1350.7 25.4 %all-gather.88.cloned.1.call-done = f32[4,256,256]{2,1,0:T(8,128)} async-done(((f32[1,256,256]{2,1,0:T(8,128)}), f32[4,256,256]{2,1,0:T(8,128)}) %all-gather.88.cloned.1.call-update) | async-done | bytes 1048592 | tf_op jit(solution)/shard_map/all_gather | solution.py:11
  (327 shorter events, 440.9 us)
Async XLA Ops:
  6.5 94.4 %copy-start = (f32[2,1,256,1,1,256]{5,4,3,2,1,0:T(1,128)S(1)}, f32[2,1,256,1,1,256]{5,4,3,2,1,0:T(1,128)}, u32[]{:S(2)}) copy-start(f32[2,1,256,1,1,256]{5,4,3,2,1,0:T(1,128)} %param.20) | copy-start | bytes 1572868
  6.5 31.9 %all-gather.56.cloned.1.call-start = ((), (), s32[]{:S(2)}) async-start(), calls=%async_computation.7 | async-start | bytes 1310720 | tf_op jit(solution)/shard_map/all_gather | solution.py:11
  8.5 141.1 %all-gather.58.cloned.1.call-start = ((), (), s32[]{:S(2)}) async-start(), calls=%async_computation.8 | async-start | bytes 4718592 | tf_op jit(solution)/shard_map/all_gather | solution.py:11
  102.6 75.7 %all-gather.60.cloned.1.call-start = ((), (), s32[]{:S(2)}) async-start(), calls=%async_computation.9 | async-start | bytes 1310720 | tf_op jit(solution)/shard_map/all_gather | solution.py:11
  152.9 54.8 %all-gather.42.cloned.1.call-start = ((), (), s32[]{:S(2)}) async-start(), calls=%async_computation | async-start | bytes 1310720 | tf_op jit(solution)/shard_map/all_gather | solution.py:11
  181.1 148.7 %all-gather.62.cloned.1.call-start = ((), (), s32[]{:S(2)}) async-start(), calls=%async_computation.10 | async-start | bytes 4718592 | tf_op jit(solution)/shard_map/all_gather | solution.py:11
  282.7 75.7 %all-gather.64.cloned.1.call-start = ((), (), s32[]{:S(2)}) async-start(), calls=%async_computation.11 | async-start | bytes 1310720 | tf_op jit(solution)/shard_map/all_gather | solution.py:11
  333.0 54.8 %all-gather.44.cloned.1.call-start = ((), (), s32[]{:S(2)}) async-start(), calls=%async_computation.1 | async-start | bytes 1310720 | tf_op jit(solution)/shard_map/all_gather | solution.py:11
  361.2 138.3 %all-gather.66.cloned.1.call-start = ((), (), s32[]{:S(2)}) async-start(), calls=%async_computation.12 | async-start | bytes 4718592 | tf_op jit(solution)/shard_map/all_gather | solution.py:11
  452.5 75.8 %all-gather.68.cloned.1.call-start = ((), (), s32[]{:S(2)}) async-start(), calls=%async_computation.13 | async-start | bytes 1310720 | tf_op jit(solution)/shard_map/all_gather | solution.py:11
  502.8 54.8 %all-gather.46.cloned.1.call-start = ((), (), s32[]{:S(2)}) async-start(), calls=%async_computation.2 | async-start | bytes 1310720 | tf_op jit(solution)/shard_map/all_gather | solution.py:11
  530.9 138.1 %all-gather.70.cloned.1.call-start = ((), (), s32[]{:S(2)}) async-start(), calls=%async_computation.14 | async-start | bytes 4718592 | tf_op jit(solution)/shard_map/all_gather | solution.py:11
  622.0 75.8 %all-gather.72.cloned.1.call-start = ((), (), s32[]{:S(2)}) async-start(), calls=%async_computation.15 | async-start | bytes 1310720 | tf_op jit(solution)/shard_map/all_gather | solution.py:11
  672.3 54.8 %all-gather.48.cloned.1.call-start = ((), (), s32[]{:S(2)}) async-start(), calls=%async_computation.3 | async-start | bytes 1310720 | tf_op jit(solution)/shard_map/all_gather | solution.py:11
  700.4 138.3 %all-gather.74.cloned.1.call-start = ((), (), s32[]{:S(2)}) async-start(), calls=%async_computation.16 | async-start | bytes 4718592 | tf_op jit(solution)/shard_map/all_gather | solution.py:11
  791.7 75.8 %all-gather.76.cloned.1.call-start = ((), (), s32[]{:S(2)}) async-start(), calls=%async_computation.17 | async-start | bytes 1310720 | tf_op jit(solution)/shard_map/all_gather | solution.py:11
  842.0 54.8 %all-gather.50.cloned.1.call-start = ((), (), s32[]{:S(2)}) async-start(), calls=%async_computation.4 | async-start | bytes 1310720 | tf_op jit(solution)/shard_map/all_gather | solution.py:11
  870.2 138.1 %all-gather.78.cloned.1.call-start = ((), (), s32[]{:S(2)}) async-start(), calls=%async_computation.18 | async-start | bytes 4718592 | tf_op jit(solution)/shard_map/all_gather | solution.py:11
  961.3 75.8 %all-gather.80.cloned.1.call-start = ((), (), s32[]{:S(2)}) async-start(), calls=%async_computation.19 | async-start | bytes 1310720 | tf_op jit(solution)/shard_map/all_gather | solution.py:11
  1011.6 54.8 %all-gather.52.cloned.1.call-start = ((), (), s32[]{:S(2)}) async-start(), calls=%async_computation.5 | async-start | bytes 1310720 | tf_op jit(solution)/shard_map/all_gather | solution.py:11
  1039.7 138.1 %all-gather.82.cloned.1.call-start = ((), (), s32[]{:S(2)}) async-start(), calls=%async_computation.20 | async-start | bytes 4718592 | tf_op jit(solution)/shard_map/all_gather | solution.py:11
  1130.8 75.8 %all-gather.84.cloned.1.call-start = ((), (), s32[]{:S(2)}) async-start(), calls=%async_computation.21 | async-start | bytes 1310720 | tf_op jit(solution)/shard_map/all_gather | solution.py:11
  1181.1 54.8 %all-gather.54.cloned.1.call-start = ((), (), s32[]{:S(2)}) async-start(), calls=%async_computation.6 | async-start | bytes 1310720 | tf_op jit(solution)/shard_map/all_gather | solution.py:11
  1209.3 138.2 %all-gather.86.cloned.1.call-start = ((), (), s32[]{:S(2)}) async-start(), calls=%async_computation.22 | async-start | bytes 4718592 | tf_op jit(solution)/shard_map/all_gather | solution.py:11
  1300.4 75.8 %all-gather.88.cloned.1.call-start = ((), (), s32[]{:S(2)}) async-start(), calls=%async_computation.23 | async-start | bytes 1310720 | tf_op jit(solution)/shard_map/all_gather | solution.py:11
Sparse Core Ops, SparseCore 0:
  9.2 29.2 all-gather.55
  102.7 46.8 all-gather.57
  153.0 25.2 all-gather.59
  181.2 26.4 all-gather.41
  282.9 46.8 all-gather.61
  333.1 25.2 all-gather.63
  361.3 26.4 all-gather.43
  452.6 46.8 all-gather.65
  502.9 25.2 all-gather.67
  531.0 26.4 all-gather.45
  622.1 46.8 all-gather.69
  672.4 25.2 all-gather.71
  700.6 26.4 all-gather.47
  791.9 46.8 all-gather.73
  842.2 25.2 all-gather.75
  870.3 26.4 all-gather.49
  961.4 46.8 all-gather.77
  1011.7 25.2 all-gather.79
  1039.8 26.4 all-gather.51
  1130.9 46.8 all-gather.81
  1181.2 25.2 all-gather.83
  1209.4 26.4 all-gather.53
  1300.5 46.8 all-gather.85
  1350.8 25.2 all-gather.87
